TPU v7x, 32 devices: a whole 2x2x4 slice. The times are simulated.
32 devices in a mesh: dp: 4 (over x, core), expert: 8 (over z, y).
Axes of the slice: x: 2, y: 2, z: 4, core: 2. Of those that a mesh axis runs over, the one named last changes fastest.
Arguments:
- tokens: bfloat16 [4096, 2048], P(('dp', 'expert')), may hold values from -6 to 6
- norm_gain: bfloat16 [2048], replicated, may hold values from 0.099609375 to 1.8984375
- router_weight: bfloat16 [2048, 8], replicated, may hold values from -0.1875 to 0.1875
- w_gate: bfloat16 [8, 2048, 5120], P('expert', None, 'dp'), may hold values from -0.125 to 0.125
- w_up: bfloat16 [8, 2048, 5120], P('expert', None, 'dp'), may hold values from -0.125 to 0.125
- w_down: bfloat16 [8, 5120, 2048], P('expert', 'dp'), may hold values from -0.078125 to 0.078125
- selected: int32 [8, 896], replicated, may hold values from 0 to 4095, as said below
Outputs:
- combined: bfloat16 [4096, 2048], P(('dp', 'expert'))
Inputs may be any that keep to these rules, and one draw needn't show every extreme that they name: `selected`: each row holds 896 distinct token indices in ascending order. Of one row's indices at most 64 fall among one device's 128 tokens and at most 336 among the tokens of one index of dp; every row reaches both bounds.
All inputs are finite; a program needn't handle non-finite values.
Results may differ from a plain program's by a relative error of at most 0.0072.
Values may be sent and summed in bfloat16 or wider, within the bound.
A program may use at most 128 MiB of HBM per device.

v0:
```python
import functools

import jax
import jax.numpy as jnp
from jax import lax
from jax.experimental import pallas as pl
from jax.experimental.pallas import tpu as pltpu
from jax.sharding import PartitionSpec as P

MESH = pl.DeviceIdType.MESH
F32 = jnp.float32
BF16 = jnp.bfloat16
CHUNKS_IN = 8
CHUNKS_OUT = 8
AHEAD = 2


def tile_of(width):
    for tile in (256, 128):
        if width % tile == 0:
            return tile
    return width


def greet(experts, chips):
    me = lax.axis_index("expert")
    dp = lax.axis_index("dp")
    chip, core = dp // 2, dp % 2
    barrier = pltpu.get_barrier_semaphore()

    half = experts // 2
    base, local = (me // half) * half, me % half

    def expert_hello(i, carry):
        pl.semaphore_signal(
            barrier, inc=1, device_id={"expert": base + (local + i) % half}, device_id_type=MESH
        )
        return carry

    lax.fori_loop(1, half, expert_hello, 0)
    pl.semaphore_signal(
        barrier, inc=1, device_id={"expert": (me + half) % experts}, device_id_type=MESH
    )
    pl.semaphore_signal(
        barrier, inc=1, device_id={"dp": 2 * chip + 1 - core}, device_id_type=MESH
    )
    for i in range(1, chips):
        pl.semaphore_signal(
            barrier,
            inc=1,
            device_id={"dp": 2 * ((chip + i) % chips) + core},
            device_id_type=MESH,
        )
    pl.semaphore_wait(barrier, half + chips)
    return me, dp, chip, core


def remote(src, dst, send_sem, recv_sem, **where):
    return pltpu.make_async_remote_copy(
        src_ref=src,
        dst_ref=dst,
        send_sem=send_sem,
        recv_sem=recv_sem,
        device_id=where,
        device_id_type=MESH,
    )


def kernel_in(
    experts, chips, chunks,
    normed, pick, pack, wg_hbm, wu_hbm, hidden,
    tok_out, tok_in, outgoing, received, rows, wg, wu, acc_g, acc_u,
    w_sem, t_send, t_recv, a_send, a_recv, x_send, s_send, b_recv,
):
    half = experts // 2
    dp_count = 2 * chips
    width = normed.shape[1] // chunks
    slots = received.shape[2]
    room = rows.shape[2]
    ff = wg.shape[1]
    tile = tile_of(ff)

    def weights(k):
        part = pl.ds(k * width, width)
        return (
            pltpu.make_async_copy(wg_hbm.at[part], wg.at[part], w_sem.at[k, 0]),
            pltpu.make_async_copy(wu_hbm.at[part], wu.at[part], w_sem.at[k, 1]),
        )

    for k in range(chunks):
        tok_out[k] = normed[:, k * width : (k + 1) * width]
    me, dp, chip, core = greet(experts, chips)
    base, local = (me // half) * half, me % half
    partner = (me + half) % experts
    sibling = 2 * chip + 1 - core

    def to_partner(k):
        return remote(
            tok_out.at[k], tok_in.at[k], t_send.at[k], t_recv.at[k], expert=partner
        )

    def to_expert(k, side, i):
        near = (local + i) % half
        owner = (me + side * half) % experts
        return remote(
            outgoing.at[k, side, near], received.at[k, owner],
            a_send.at[k, side, near], a_recv.at[k, owner], expert=base + near,
        )

    def from_expert(k, side, i):
        near = (local + i) % half
        owner = (base + near + side * half) % experts
        return remote(
            outgoing.at[k, side, near], received.at[k, owner],
            a_send.at[k, side, near], a_recv.at[k, owner], expert=base + near,
        )

    def to_chip(k, i):
        other = 2 * ((chip + i) % chips) + core
        return remote(
            rows.at[k, dp], rows.at[k, dp], x_send.at[k, i], b_recv.at[k, dp], dp=other
        )

    def from_chip(k, i):
        other = 2 * ((chip + i) % chips) + core
        return remote(
            rows.at[k, other], rows.at[k, other], x_send.at[k, i], b_recv.at[k, other], dp=other
        )

    def to_sibling(k, i):
        block = 2 * ((chip + i) % chips) + core
        return remote(
            rows.at[k, block], rows.at[k, block], s_send.at[k, i], b_recv.at[k, block],
            dp=sibling,
        )

    def from_sibling(k, i):
        block = 2 * ((chip + i) % chips) + 1 - core
        return remote(
            rows.at[k, block], rows.at[k, block], s_send.at[k, i], b_recv.at[k, block],
            dp=sibling,
        )

    def send_rows(k, side, source):
        chosen = jnp.dot(pick[side], source, preferred_element_type=F32)
        outgoing[k, side] = chosen.astype(BF16).reshape(half, slots, width)

        def send(i, carry):
            to_expert(k, side, i).start()
            return carry

        lax.fori_loop(1, half, send, 0)
        received[k, (me + side * half) % experts] = outgoing[k, side, local]

    for k in range(min(AHEAD, chunks)):
        to_partner(k).start()
    send_rows(0, 0, tok_out[0])
    for k in range(chunks):
        for copy in weights(k):
            copy.start()

    for step in range(chunks + 3):
        if step + AHEAD < chunks:
            to_partner(step + AHEAD).start()
        if step + 1 < chunks:
            send_rows(step + 1, 0, tok_out[step + 1])
        if step < chunks:
            to_partner(step).wait_recv()
            send_rows(step, 1, tok_in[step])
        if 1 <= step <= chunks:
            k = step - 1

            def take(i, carry):
                from_expert(k, 0, i).wait_recv()
                from_expert(k, 1, i).wait_recv()
                return carry

            lax.fori_loop(1, half, take, 0)
            packed = jnp.dot(
                pack[...],
                received[k].reshape(experts * slots, width),
                preferred_element_type=F32,
            )
            rows[k, dp] = packed.astype(BF16)
            for i in range(1, chips):
                to_chip(k, i).start()
            to_sibling(k, 0).start()
        if 2 <= step <= chunks + 1:
            for i in range(1, chips):
                from_chip(step - 2, i).wait_recv()
                to_sibling(step - 2, i).start()
        if step >= 3:
            k = step - 3
            for i in range(chips):
                from_sibling(k, i).wait_recv()
            for copy in weights(k):
                copy.wait()

            def multiply(n, carry):
                cols = pl.ds(pl.multiple_of(n * tile, tile), tile)
                depth = pl.ds(k * width, width)
                block = rows[k].reshape(dp_count * room, width)
                g = jnp.dot(block, wg[depth, cols], preferred_element_type=F32)
                u = jnp.dot(block, wu[depth, cols], preferred_element_type=F32)
                if k > 0:
                    g = g + acc_g[:, cols]
                    u = u + acc_u[:, cols]
                if k < chunks - 1:
                    acc_g[:, cols] = g
                    acc_u[:, cols] = u
                else:
                    hidden[:, cols] = (jax.nn.gelu(g, approximate=True) * u).astype(BF16)
                return carry

            lax.fori_loop(0, ff // tile, multiply, 0)

    for k in range(chunks):
        to_partner(k).wait_send()

        def sent(i, carry):
            to_expert(k, 0, i).wait_send()
            to_expert(k, 1, i).wait_send()
            return carry

        lax.fori_loop(1, half, sent, 0)
        for i in range(1, chips):
            to_chip(k, i).wait_send()
        for i in range(chips):
            to_sibling(k, i).wait_send()


def kernel_out(
    experts, chips, chunks,
    hidden, unpack, mixing, wd_hbm, out,
    wd, own, sib_out, sib_in, x_out, x_in, returning, arrived, tok_out, tok_in,
    mix_high, mix_low,
    w_sem, s_send, s_recv, x_send, x_recv, a_send, a_recv, t_send, t_recv,
):
    half = experts // 2
    width = out.shape[1] // chunks
    slots = arrived.shape[3]

    def weights(k):
        part = pl.ds(k * width, width)
        return pltpu.make_async_copy(wd_hbm.at[:, part], wd.at[k], w_sem.at[k])

    for k in range(chunks):
        weights(k).start()
    me, dp, chip, core = greet(experts, chips)
    base, local = (me // half) * half, me % half
    partner = (me + half) % experts
    sibling = 2 * chip + 1 - core
    high = mixing[...].astype(BF16)
    mix_high[...] = high
    mix_low[...] = (mixing[...] - high.astype(F32)).astype(BF16)

    def sib_copy(k, i):
        return remote(
            sib_out.at[k, i], sib_in.at[k, i], s_send.at[k, i], s_recv.at[k, i], dp=sibling
        )

    def chip_copy(k, i):
        return remote(
            x_out.at[k, i - 1], x_in.at[k, i - 1], x_send.at[k, i - 1], x_recv.at[k, i - 1],
            dp=2 * ((chip + i) % chips) + core,
        )

    def to_expert(k, side, i):
        near = (local + i) % half
        owner = (base + near + side * half) % experts
        return remote(
            returning.at[k, owner], arrived.at[k, side, local],
            a_send.at[k, owner], a_recv.at[k, side, local], expert=base + near,
        )

    def from_expert(k, side, i):
        near = (local + i) % half
        owner = (base + near + side * half) % experts
        return remote(
            returning.at[k, owner], arrived.at[k, side, near],
            a_send.at[k, owner], a_recv.at[k, side, near], expert=base + near,
        )

    def to_partner(k):
        return remote(
            tok_out.at[k], tok_in.at[k], t_send.at[k], t_recv.at[k], expert=partner
        )

    def mixed(k, side):
        values = arrived[k, side].reshape(half * slots, width)
        sums = jnp.dot(mix_high[side], values, preferred_element_type=F32)
        return sums + jnp.dot(mix_low[side], values, preferred_element_type=F32)

    def take_side(k, side):
        def take(i, carry):
            from_expert(k, side, i).wait_recv()
            return carry

        lax.fori_loop(1, half, take, 0)

    for step in range(chunks + 4):
        if step < chunks:
            k = step
            weights(k).wait()

            def give(i, carry):
                block = 2 * ((chip + i) % chips) + 1 - core
                term = jnp.dot(hidden[block], wd[k], preferred_element_type=F32)
                sib_out[k, i] = term.astype(BF16)
                sib_copy(k, i).start()
                return carry

            lax.fori_loop(0, chips, give, 0)

            def keep(i, carry):
                block = 2 * ((chip + i) % chips) + core
                own[k, i] = jnp.dot(hidden[block], wd[k], preferred_element_type=F32)
                return carry

            lax.fori_loop(0, chips, keep, 0)
        if 1 <= step <= chunks:
            k = step - 1
            for i in range(chips):
                sib_copy(k, i).wait_recv()
            for i in range(1, chips):
                x_out[k, i - 1] = (own[k, i] + sib_in[k, i].astype(F32)).astype(BF16)
                chip_copy(k, i).start()
        if 2 <= step <= chunks + 1:
            k = step - 2
            total = own[k, 0] + sib_in[k, 0].astype(F32)
            for i in range(1, chips):
                chip_copy(k, i).wait_recv()
                total = total + x_in[k, i - 1].astype(F32)
            spread = jnp.dot(unpack[...], total.astype(BF16), preferred_element_type=F32)
            returning[k] = spread.astype(BF16).reshape(experts, slots, width)
            for side in (1, 0):

                def send(i, carry):
                    to_expert(k, side, i).start()
                    return carry

                lax.fori_loop(1, half, send, 0)
                arrived[k, side, local] = returning[k, (me + side * half) % experts]
        if 3 <= step <= chunks + 2:
            k = step - 3
            take_side(k, 1)
            tok_out[k] = mixed(k, 1).astype(BF16)
            to_partner(k).start()
        if step >= 4:
            k = step - 4
            take_side(k, 0)
            near_sum = mixed(k, 0)
            to_partner(k).wait_recv()
            combined = near_sum + tok_in[k].astype(F32)
            out[:, k * width : (k + 1) * width] = combined.astype(BF16)

    for k in range(chunks):
        for i in range(chips):
            sib_copy(k, i).wait_send()
        for i in range(1, chips):
            chip_copy(k, i).wait_send()
        to_partner(k).wait_send()

        def sent(i, carry):
            to_expert(k, 0, i).wait_send()
            to_expert(k, 1, i).wait_send()
            return carry

        lax.fori_loop(1, half, sent, 0)


def per_device(tokens, norm_gain, router_weight, w_gate, w_up, w_down, selected):
    dp_count = lax.axis_size("dp")
    experts = lax.axis_size("expert")
    chips = dp_count // 2
    tok_rows, model_width = tokens.shape
    capacity = selected.shape[1]
    ff = w_gate.shape[2]
    slots = 4 * tok_rows // experts
    room = 3 * capacity // (2 * dp_count)
    dp_index = lax.axis_index("dp")
    expert_index = lax.axis_index("expert")
    activations = tokens.astype(F32)
    mean_square = jnp.mean(activations * activations, axis=1, keepdims=True)
    normed = (activations * lax.rsqrt(mean_square + 1e-06) * norm_gain.astype(F32)).astype(BF16)
    gate_probs = jax.nn.sigmoid(jnp.dot(normed, router_weight, preferred_element_type=F32))

    half = experts // 2
    base = (expert_index // half) * half
    partner = (expert_index + half) % experts
    near = lax.dynamic_slice_in_dim(selected, base, half, 0)
    pair = dp_index * experts + jnp.stack([expert_index, partner])
    order = jnp.arange(tok_rows, dtype=jnp.int32)
    ours = (pair[:, None] * tok_rows + order[None, :]).reshape(-1)
    member = jnp.any(near[:, :, None] == ours[None, None, :], axis=1)
    member = member.reshape(half * 2, tok_rows)
    before = (order[:, None] < order[None, :]).astype(BF16)
    rank = jnp.dot(member.astype(BF16), before, preferred_element_type=F32)
    slot = jnp.arange(slots, dtype=F32)
    place = jnp.where(member, rank, -1.0).reshape(half, 2, tok_rows).transpose(1, 0, 2)
    chosen = place[:, :, None, :] == slot[None, None, :, None]
    pick = chosen.astype(BF16).reshape(2, half * slots, tok_rows)
    swap = [(e, (e + half) % experts) for e in range(experts)]
    far_probs = lax.ppermute(gate_probs, "expert", swap)
    probs = lax.dynamic_slice_in_dim(jnp.stack([gate_probs, far_probs]), base, half, 2)
    placed = place.transpose(0, 2, 1)
    mixing = jnp.where(
        placed[:, :, :, None] == slot[None, None, None, :], probs[:, :, :, None], 0.0
    ).reshape(2, tok_rows, half * slots)

    expert_row = lax.dynamic_index_in_dim(selected, expert_index, 0, keepdims=False)
    senders = jnp.arange(experts, dtype=jnp.int32)
    first_token = (dp_index * experts + senders) * tok_rows
    firsts = jnp.sum((expert_row[None, :] < first_token[:, None]).astype(jnp.int32), axis=1)
    lasts = jnp.sum(
        (expert_row[None, :] < first_token[:, None] + tok_rows).astype(jnp.int32), axis=1
    )
    places = jnp.arange(slots, dtype=jnp.int32)
    target = jnp.where(
        places[None, :] < (lasts - firsts)[:, None],
        (firsts - firsts[0])[:, None] + places[None, :],
        -1,
    ).reshape(-1)
    spots = jnp.arange(room, dtype=jnp.int32)
    pack = (spots[:, None] == target[None, :]).astype(BF16)
    unpack = (target[:, None] == spots[None, :]).astype(BF16)

    in_vmem = pl.BlockSpec(memory_space=pltpu.VMEM)
    in_any = pl.BlockSpec(memory_space=pl.ANY)
    dma = pltpu.SemaphoreType.DMA
    all_rows = dp_count * room
    chunks = CHUNKS_IN
    width = model_width // chunks
    hidden = pl.pallas_call(
        functools.partial(kernel_in, experts, chips, chunks),
        out_shape=jax.ShapeDtypeStruct((all_rows, ff), BF16),
        in_specs=[in_vmem, in_vmem, in_vmem, in_any, in_any],
        out_specs=in_vmem,
        scratch_shapes=[
            pltpu.VMEM((chunks, tok_rows, width), BF16),
            pltpu.VMEM((chunks, tok_rows, width), BF16),
            pltpu.VMEM((chunks, 2, half, slots, width), BF16),
            pltpu.VMEM((chunks, experts, slots, width), BF16),
            pltpu.VMEM((chunks, dp_count, room, width), BF16),
            pltpu.VMEM((model_width, ff), BF16),
            pltpu.VMEM((model_width, ff), BF16),
            pltpu.VMEM((all_rows, ff), F32),
            pltpu.VMEM((all_rows, ff), F32),
            dma((chunks, 2)),
            dma((chunks,)),
            dma((chunks,)),
            dma((chunks, 2, half)),
            dma((chunks, experts)),
            dma((chunks, chips)),
            dma((chunks, chips)),
            dma((chunks, dp_count)),
        ],
        compiler_params=pltpu.CompilerParams(
            collective_id=0, has_side_effects=True, vmem_limit_bytes=60 * 2**20
        ),
        name="dispatch",
    )(normed, pick, pack, w_gate[0], w_up[0])

    chunks = CHUNKS_OUT
    width = model_width // chunks
    return pl.pallas_call(
        functools.partial(kernel_out, experts, chips, chunks),
        out_shape=jax.ShapeDtypeStruct((tok_rows, model_width), BF16),
        in_specs=[in_vmem, in_vmem, in_vmem, in_any],
        out_specs=in_vmem,
        scratch_shapes=[
            pltpu.VMEM((chunks, ff, width), BF16),
            pltpu.VMEM((chunks, chips, room, width), F32),
            pltpu.VMEM((chunks, chips, room, width), BF16),
            pltpu.VMEM((chunks, chips, room, width), BF16),
            pltpu.VMEM((chunks, max(chips - 1, 1), room, width), BF16),
            pltpu.VMEM((chunks, max(chips - 1, 1), room, width), BF16),
            pltpu.VMEM((chunks, experts, slots, width), BF16),
            pltpu.VMEM((chunks, 2, half, slots, width), BF16),
            pltpu.VMEM((chunks, tok_rows, width), BF16),
            pltpu.VMEM((chunks, tok_rows, width), BF16),
            pltpu.VMEM((2, tok_rows, half * slots), BF16),
            pltpu.VMEM((2, tok_rows, half * slots), BF16),
            dma((chunks,)),
            dma((chunks, chips)),
            dma((chunks, chips)),
            dma((chunks, max(chips - 1, 1))),
            dma((chunks, max(chips - 1, 1))),
            dma((chunks, experts)),
            dma((chunks, 2, half)),
            dma((chunks,)),
            dma((chunks,)),
        ],
        compiler_params=pltpu.CompilerParams(
            collective_id=1, has_side_effects=True, vmem_limit_bytes=60 * 2**20
        ),
        name="combine",
    )(hidden.reshape(dp_count, room, ff), unpack, mixing, w_down[0])


def solution(mesh):
    in_specs = (
        P(("dp", "expert"), None),
        P(),
        P(),
        P("expert", None, "dp"),
        P("expert", None, "dp"),
        P("expert", "dp", None),
        P(),
    )
    out_specs = P(("dp", "expert"), None)
    return jax.shard_map(
        per_device, mesh=mesh, in_specs=in_specs, out_specs=out_specs, check_vma=False
    )
```

profile of v0, /device:TPU:0, one launch (start us, length us, event | category | flops | bytes accessed | tf_op | source)
XLA Modules:
  0.0 135.5 jit_solution(786902803163369527)
XLA Ops:
  0.0 0.0 copy-start
  0.0 0.7 convert_element_type.28
  0.7 1.2 fusion.3
  1.9 1.2 fusion.5.normed
  3.2 0.0 copy-done
  3.2 0.0 copy-start.1
  3.2 0.2 fusion.2
  3.4 4.1 %collective-permute-start = (f32[128,8]{0,1:T(8,128)S(1)}, f32[128,8]{0,1:T(8,128)S(1)}, u32[]{:S(2)}, u32[]{:S(2)}) collective-permute-start(f32[128,8]{0,1:T(8,128)S(1)} %fusion.2), channel_id=1, source_target_pairs={{0,4},{1,5},{2,6},{3,7},{4,0},{5,1},{6,2},{7,3},{8,12},{9,13},{10,... | collective-permute-start | bytes 12296 | tf_op jit(solution)/shard_map/ppermute | solution.py:404
  7.5 0.8 dynamic-slice_reduce_fusion
  8.3 0.2 convert_reduce_fusion.1
  8.5 0.1 fusion.11
  8.6 0.1 add_select_fusion
  8.7 0.1 select_n.49
  8.7 0.8 fusion.7.pack
  9.5 0.9 fusion.6.unpack
  10.4 0.8 constant_dynamic-slice_fusion
  11.2 0.1 fusion.10
  11.3 0.1 add_bitcast_fusion
  11.3 0.6 compare_reduce_fusion
  12.0 0.1 convolution_select_fusion
  12.1 0.1 eq.87
  12.3 0.1 copy.17
  12.4 0.8 fusion.8.pick
  13.2 0.0 copy-done.1
  13.2 62.6 %dispatch.1 = bf16[1344,1280]{1,0:T(8,128)(2,1)} custom-call(bf16[128,2048]{1,0:T(8,128)(2,1)} %copy-done.1, bf16[2,256,128]{2,1,0:T(8,128)(2,1)} %fusion.8.pick, bf16[336,512]{1,0:T(8,128)(2,1)} %fusion.7.pack, bf16[2048,1280]{1,0:T(8,128)(2,1)} %bitcast.27, bf16[2048,1280]{1,0:T(8,128)(2,1)} %bitcast.28), custom_call_target="tpu_custom_call" | custom-call | tf_op jit(solution)/shard_map/dispatch/pallas_call | solution.py:434
  75.8 0.0 collective-permute-done
  75.8 0.1 copy.18
  76.0 0.7 compare_select_fusion.mixing
  76.7 56.9 %combine.1 = bf16[128,2048]{1,0:T(8,128)(2,1)} custom-call(bf16[4,336,1280]{2,1,0:T(8,128)(2,1)} %bitcast.26, bf16[512,336]{1,0:T(8,128)(2,1)} %fusion.6.unpack, f32[2,128,256]{2,1,0:T(8,128)} %compare_select_fusion.mixing, bf16[1280,2048]{1,0:T(8,128)(2,1)} %bitcast.29), custom_call_target="tpu_custom_call" | custom-call | tf_op jit(solution)/shard_map/combine/pallas_call | solution.py:466
  133.6 1.9 %copy.20 = bf16[128,2048]{1,0:T(8,128)(2,1)} copy(bf16[128,2048]{1,0:T(8,128)(2,1)} %combine.1) | data formatting | bytes 1048576
  (9 shorter events, 0.1 us)
Async XLA Ops:
  0.0 3.2 %copy-start = (bf16[2048,8]{0,1:T(8,128)(2,1)S(1)}, bf16[2048,8]{0,1:T(8,128)(2,1)}, u32[]{:S(2)}) copy-start(bf16[2048,8]{0,1:T(8,128)(2,1)} %param.9) | copy-start | bytes 98308
  3.2 10.0 %copy-start.1 = (bf16[128,2048]{1,0:T(8,128)(2,1)}, bf16[128,2048]{1,0:T(8,128)(2,1)S(1)}, u32[]{:S(2)}) copy-start(bf16[128,2048]{1,0:T(8,128)(2,1)S(1)} %fusion.5.normed) | copy-start | bytes 1572868
  3.4 72.4 %collective-permute-start = (f32[128,8]{0,1:T(8,128)S(1)}, f32[128,8]{0,1:T(8,128)S(1)}, u32[]{:S(2)}, u32[]{:S(2)}) collective-permute-start(f32[128,8]{0,1:T(8,128)S(1)} %fusion.2), channel_id=1, source_target_pairs={{0,4},{1,5},{2,6},{3,7},{4,0},{5,1},{6,2},{7,3},{8,12},{9,13},{10,... | collective-permute-start | bytes 12296 | tf_op jit(solution)/shard_map/ppermute | solution.py:404
where the time goes:
time: 136 us; the launch traced here: 135 us
  Pallas kernels  120 us (88%)
  other arithmetic  7.5 us (6%)
  starting transfers between devices  4.09 us (3%)
  local copies, waits for them, and re-layouts  3.9 us (3%)
    pallas_call x1, Pallas kernels, per_device(): pl.pallas_call(functools.partial(kernel_in, experts, chips, chunks), out_...  62.6 us
    pallas_call x1, Pallas kernels, per_device(): pl.pallas_call(functools.partial(kernel_out, experts, chips, chunks), out...  56.9 us
    ppermute x1, starting transfers between devices, per_device(): far_probs = lax.ppermute(gate_probs, 'expert', swap)  4.09 us
  transfers between devices with their start and end apart: 1, of which 0 were waited for; matrix products, arithmetic and copies ran while one was open for 4% of the time, Pallas kernels for 46%

commit v1 on v0

v1 whole, which is shorter than its diff:
```python
import functools

import jax
import jax.numpy as jnp
from jax import lax
from jax.experimental import pallas as pl
from jax.experimental.pallas import tpu as pltpu
from jax.sharding import PartitionSpec as P

MESH = pl.DeviceIdType.MESH
F32 = jnp.float32
BF16 = jnp.bfloat16
CHUNKS = 8
AHEAD = 2
NEAR_LAG, CHIP_LAG, CORE_LAG = 2, 2, 1
SIB_LAG, X_LAG, BACK_LAG, PAIR_LAG = 1, 2, 2, 2


def tile_of(width):
    for tile in (256, 128):
        if width % tile == 0:
            return tile
    return width


def remote(src, dst, send_sem, recv_sem, **where):
    return pltpu.make_async_remote_copy(
        src_ref=src,
        dst_ref=dst,
        send_sem=send_sem,
        recv_sem=recv_sem,
        device_id=where,
        device_id_type=MESH,
    )


def iota(shape, axis):
    return lax.broadcasted_iota(jnp.int32, shape, axis)


def kernel(
    experts, chips, chunks,
    tokens_hbm, gain_hbm, router_hbm, selected_hbm, wg_hbm, wu_hbm, wd_hbm, out,
    tokens, gain, router, selected, chosen, pick, pack, unpack, mix_high, mix_low,
    tok_out, tok_in, outgoing, received, rows, wg, wu, wd, acc_g, acc_u, hidden,
    sib_in, x_in, returning, arrived, back_out, back_in,
    i_sem, w_sem, d_sem, t_send, t_recv, a_send, a_recv, x_send, s_send, b_recv,
    c_send, c_recv, o_send, o_recv, r_send, r_recv, p_send, p_recv,
):
    half = experts // 2
    dp_count = 2 * chips
    tok_rows = tokens.shape[0]
    width = tok_out.shape[2]
    slots = received.shape[2]
    room = rows.shape[2]
    capacity = selected.shape[1]
    ff = wg.shape[1]
    tile = tile_of(ff)
    lanes = half * slots

    me = lax.axis_index("expert")
    dp = lax.axis_index("dp")
    chip, core = dp // 2, dp % 2
    base, local = (me // half) * half, me % half
    partner = (me + half) % experts
    sibling = 2 * chip + 1 - core

    loads = [
        pltpu.make_async_copy(src, dst, i_sem.at[i])
        for i, (src, dst) in enumerate(
            (
                (tokens_hbm, tokens),
                (gain_hbm, gain),
                (selected_hbm, selected.at[pl.ds(0, experts)]),
                (router_hbm, router),
            )
        )
    ]
    for copy in loads:
        copy.start()

    barrier = pltpu.get_barrier_semaphore()

    def expert_hello(i, carry):
        pl.semaphore_signal(
            barrier, inc=1, device_id={"expert": base + (local + i) % half}, device_id_type=MESH
        )
        return carry

    lax.fori_loop(1, half, expert_hello, 0)
    pl.semaphore_signal(barrier, inc=1, device_id={"expert": partner}, device_id_type=MESH)
    pl.semaphore_signal(barrier, inc=1, device_id={"dp": sibling}, device_id_type=MESH)
    for i in range(1, chips):
        pl.semaphore_signal(
            barrier,
            inc=1,
            device_id={"dp": 2 * ((chip + i) % chips) + core},
            device_id_type=MESH,
        )

    def weights(k):
        part = pl.ds(k * width, width)
        return (
            pltpu.make_async_copy(wg_hbm.at[part], wg.at[part], w_sem.at[k, 0]),
            pltpu.make_async_copy(wu_hbm.at[part], wu.at[part], w_sem.at[k, 1]),
        )

    def down_weights(k):
        part = pl.ds(k * width, width)
        return pltpu.make_async_copy(wd_hbm.at[:, part], wd.at[k], d_sem.at[k])

    loads[0].wait()
    loads[1].wait()
    for k in range(chunks):
        for copy in weights(k):
            copy.start()
    for k in range(chunks):
        down_weights(k).start()
    activations = tokens[...].astype(F32)
    mean_square = jnp.mean(activations * activations, axis=1, keepdims=True)
    scale = lax.rsqrt(mean_square + 1e-06)
    for k in range(chunks):
        part = slice(k * width, (k + 1) * width)
        tok_out[k] = (
            tokens[:, part].astype(F32) * scale * gain[:, part].astype(F32)
        ).astype(BF16)
    pl.semaphore_wait(barrier, half + chips)

    def to_partner(k):
        return remote(
            tok_out.at[k], tok_in.at[k], t_send.at[k], t_recv.at[k], expert=partner
        )

    def to_expert(k, side, i):
        near = (local + i) % half
        owner = (me + side * half) % experts
        return remote(
            outgoing.at[k, side, near], received.at[k, owner],
            a_send.at[k, side, near], a_recv.at[k, owner], expert=base + near,
        )

    def from_expert(k, side, i):
        near = (local + i) % half
        owner = (base + near + side * half) % experts
        return remote(
            outgoing.at[k, side, near], received.at[k, owner],
            a_send.at[k, side, near], a_recv.at[k, owner], expert=base + near,
        )

    def to_chip(k, i):
        other = 2 * ((chip + i) % chips) + core
        return remote(
            rows.at[k, dp], rows.at[k, dp], x_send.at[k, i], b_recv.at[k, dp], dp=other
        )

    def from_chip(k, i):
        other = 2 * ((chip + i) % chips) + core
        return remote(
            rows.at[k, other], rows.at[k, other], x_send.at[k, i], b_recv.at[k, other], dp=other
        )

    def to_sibling(k, i):
        block = 2 * ((chip + i) % chips) + core
        return remote(
            rows.at[k, block], rows.at[k, block], s_send.at[k, i], b_recv.at[k, block],
            dp=sibling,
        )

    def from_sibling(k, i):
        block = 2 * ((chip + i) % chips) + 1 - core
        return remote(
            rows.at[k, block], rows.at[k, block], s_send.at[k, i], b_recv.at[k, block],
            dp=sibling,
        )

    for k in range(min(AHEAD, chunks)):
        to_partner(k).start()
    loads[2].wait()
    loads[3].wait()

    spot = iota((1, capacity), 1).astype(F32)
    lane = iota((1, lanes), 1).astype(F32)

    def choose(side):
        first = (dp * experts + (me + side * half) % experts) * tok_rows
        ids = first + iota((tok_rows, 1), 0)
        total = jnp.zeros((tok_rows, lanes), F32)
        for e in range(half):
            row = selected[pl.ds(base + e, 1), :]
            at = jnp.max(jnp.where(row == ids, spot, -1.0), axis=1, keepdims=True)
            begin = jnp.sum(jnp.where(row < first, 1.0, 0.0), axis=1, keepdims=True)
            goal = jnp.where(at >= 0.0, at - begin + float(e * slots), -1.0)
            total = total + jnp.where(goal == lane, 1.0, 0.0)
        chosen[side] = total.astype(BF16)
        pick[side] = total.T.astype(BF16)

    def send_rows(k, side, source):
        picked = jnp.dot(pick[side], source, preferred_element_type=F32)
        outgoing[k, side] = picked.astype(BF16).reshape(half, slots, width)

        def send(i, carry):
            to_expert(k, side, i).start()
            return carry

        lax.fori_loop(1, half, send, 0)
        received[k, (me + side * half) % experts] = outgoing[k, side, local]

    choose(0)
    send_rows(0, 0, tok_out[0])
    choose(1)

    mine = selected[pl.ds(me, 1), :]
    starts = (dp * experts + iota((experts + 8, 1), 0)) * tok_rows
    firsts = jnp.sum(jnp.where(mine < starts, 1.0, 0.0), axis=1, keepdims=True)
    place = iota((1, experts * slots), 1).astype(F32)
    target = jnp.full((1, experts * slots), -1.0, F32)
    slot = iota((slots, 1), 0).astype(F32)
    seats = iota((1, room), 1).astype(F32)
    for j in range(experts):
        offset = firsts[j : j + 1] - firsts[0:1]
        count = firsts[j + 1 : j + 2] - firsts[j : j + 1]
        within = place - float(j * slots)
        here = jnp.logical_and(within >= 0.0, within < count)
        target = jnp.where(here, within + offset, target)
        goal = jnp.where(slot < count, slot + offset, -1.0)
        unpack[j * slots : (j + 1) * slots, :] = jnp.where(goal == seats, 1.0, 0.0).astype(BF16)
    seat = iota((room, 1), 0).astype(F32)
    pack[...] = jnp.where(seat == target, 1.0, 0.0).astype(BF16)

    def weigh(side, source):
        logits = jnp.zeros((tok_rows, experts), F32)
        for k in range(chunks):
            logits = logits + lax.dot_general(
                source[k], router[:, k * width : (k + 1) * width],
                (((1,), (1,)), ((), ())), preferred_element_type=F32,
            )
        probs = jax.nn.sigmoid(logits)
        column = iota((1, experts), 1)
        spread = jnp.zeros((tok_rows, lanes), F32)
        for e in range(half):
            prob = jnp.sum(jnp.where(column == base + e, probs, 0.0), axis=1, keepdims=True)
            inside = jnp.logical_and(lane >= float(e * slots), lane < float((e + 1) * slots))
            spread = jnp.where(inside, prob, spread)
        mixing = jnp.where(chosen[side].astype(F32) > 0.5, spread, 0.0)
        high = mixing.astype(BF16)
        mix_high[side] = high
        mix_low[side] = (mixing - high.astype(F32)).astype(BF16)

    lag_x = NEAR_LAG + CHIP_LAG
    lag_m = lag_x + CORE_LAG
    for step in range(chunks + lag_m):
        if step < chunks:
            to_partner(step).wait_recv()
            send_rows(step, 1, tok_in[step])
        if step + AHEAD < chunks:
            to_partner(step + AHEAD).start()
        if step + 1 < chunks:
            send_rows(step + 1, 0, tok_out[step + 1])
        if NEAR_LAG <= step < chunks + NEAR_LAG:
            k = step - NEAR_LAG

            def take(i, carry):
                from_expert(k, 0, i).wait_recv()
                from_expert(k, 1, i).wait_recv()
                return carry

            lax.fori_loop(1, half, take, 0)
            packed = jnp.dot(
                pack[...],
                received[k].reshape(experts * slots, width),
                preferred_element_type=F32,
            )
            rows[k, dp] = packed.astype(BF16)
            for i in range(1, chips):
                to_chip(k, i).start()
            to_sibling(k, 0).start()
        if lag_x <= step < chunks + lag_x:
            k = step - lag_x
            for i in range(1, chips):
                from_chip(k, i).wait_recv()
                to_sibling(k, i).start()
        if step == chunks:
            weigh(0, tok_out)
            weigh(1, tok_in)
        if step >= lag_m:
            k = step - lag_m
            for i in range(chips):
                from_sibling(k, i).wait_recv()
            for copy in weights(k):
                copy.wait()

            def multiply(n, carry):
                cols = pl.ds(pl.multiple_of(n * tile, tile), tile)
                depth = pl.ds(k * width, width)
                block = rows[k].reshape(dp_count * room, width)
                g = jnp.dot(block, wg[depth, cols], preferred_element_type=F32)
                u = jnp.dot(block, wu[depth, cols], preferred_element_type=F32)
                if k > 0:
                    g = g + acc_g[:, cols]
                    u = u + acc_u[:, cols]
                if k < chunks - 1:
                    acc_g[:, cols] = g
                    acc_u[:, cols] = u
                else:
                    hidden[:, cols] = (jax.nn.gelu(g, approximate=True) * u).astype(BF16)
                return carry

            lax.fori_loop(0, ff // tile, multiply, 0)

    places = ff // width

    def own(k, i):
        at = k % (2 * places)
        row = ((at // places) * chips + i) * room
        return acc_g.at[pl.ds(row, room), pl.ds((at % places) * width, width)]

    def sib_copy(k, i):
        return remote(
            rows.at[k, i], sib_in.at[k, i], c_send.at[k, i], c_recv.at[k, i], dp=sibling
        )

    def chip_copy(k, i):
        return remote(
            rows.at[k, chips + i - 1], x_in.at[k, i - 1],
            o_send.at[k, i - 1], o_recv.at[k, i - 1],
            dp=2 * ((chip + i) % chips) + core,
        )

    def give_back(k, side, i):
        near = (local + i) % half
        owner = (base + near + side * half) % experts
        return remote(
            returning.at[k, owner], arrived.at[k, side, local],
            r_send.at[k, owner], r_recv.at[k, side, local], expert=base + near,
        )

    def take_back(k, side, i):
        near = (local + i) % half
        owner = (base + near + side * half) % experts
        return remote(
            returning.at[k, owner], arrived.at[k, side, near],
            r_send.at[k, owner], r_recv.at[k, side, near], expert=base + near,
        )

    def pair_copy(k):
        return remote(
            back_out.at[k], back_in.at[k], p_send.at[k], p_recv.at[k], expert=partner
        )

    def mixed(k, side):
        values = arrived[k, side].reshape(half * slots, width)
        sums = jnp.dot(mix_high[side], values, preferred_element_type=F32)
        return sums + jnp.dot(mix_low[side], values, preferred_element_type=F32)

    def take_side(k, side):
        def take(i, carry):
            take_back(k, side, i).wait_recv()
            return carry

        lax.fori_loop(1, half, take, 0)

    def block_rows(block):
        return hidden[pl.ds(pl.multiple_of(block * room, 16), room), :]

    lag_t = SIB_LAG + X_LAG
    lag_b = lag_t + BACK_LAG
    lag_p = lag_b + PAIR_LAG
    for step in range(chunks + lag_p):
        if step < chunks:
            k = step
            down_weights(k).wait()
            for i in range(1, chips):
                to_chip(k, i).wait_send()
            for i in range(chips):
                to_sibling(k, i).wait_send()

            def give(i, carry):
                block = 2 * ((chip + i) % chips) + 1 - core
                term = jnp.dot(block_rows(block), wd[k], preferred_element_type=F32)
                rows[k, i] = term.astype(BF16)
                sib_copy(k, i).start()
                return carry

            lax.fori_loop(0, chips, give, 0)

            def keep(i, carry):
                block = 2 * ((chip + i) % chips) + core
                own(k, i)[...] = jnp.dot(block_rows(block), wd[k], preferred_element_type=F32)
                return carry

            lax.fori_loop(0, chips, keep, 0)
        if SIB_LAG <= step < chunks + SIB_LAG:
            k = step - SIB_LAG
            for i in range(chips):
                sib_copy(k, i).wait_recv()
            for i in range(1, chips):
                rows[k, chips + i - 1] = (own(k, i)[...] + sib_in[k, i].astype(F32)).astype(BF16)
                chip_copy(k, i).start()
        if lag_t <= step < chunks + lag_t:
            k = step - lag_t
            total = own(k, 0)[...] + sib_in[k, 0].astype(F32)
            for i in range(1, chips):
                chip_copy(k, i).wait_recv()
                total = total + x_in[k, i - 1].astype(F32)
            spread = jnp.dot(unpack[...], total.astype(BF16), preferred_element_type=F32)
            returning[k] = spread.astype(BF16).reshape(experts, slots, width)
            for side in (1, 0):

                def send(i, carry):
                    give_back(k, side, i).start()
                    return carry

                lax.fori_loop(1, half, send, 0)
                arrived[k, side, local] = returning[k, (me + side * half) % experts]
        if lag_b <= step < chunks + lag_b:
            k = step - lag_b
            take_side(k, 1)
            back_out[k] = mixed(k, 1).astype(BF16)
            pair_copy(k).start()
        if step >= lag_p:
            k = step - lag_p
            take_side(k, 0)
            near_sum = mixed(k, 0)
            pair_copy(k).wait_recv()
            combined = near_sum + back_in[k].astype(F32)
            out[:, k * width : (k + 1) * width] = combined.astype(BF16)

    for k in range(chunks):
        to_partner(k).wait_send()

        def sent(i, carry):
            for side in (0, 1):
                to_expert(k, side, i).wait_send()
                give_back(k, side, i).wait_send()
            return carry

        lax.fori_loop(1, half, sent, 0)
        for i in range(chips):
            sib_copy(k, i).wait_send()
        for i in range(1, chips):
            chip_copy(k, i).wait_send()
        pair_copy(k).wait_send()


def per_device(tokens, norm_gain, router_weight, w_gate, w_up, w_down, selected):
    dp_count = lax.axis_size("dp")
    experts = lax.axis_size("expert")
    chips = dp_count // 2
    tok_rows, model_width = tokens.shape
    capacity = selected.shape[1]
    ff = w_gate.shape[2]
    slots = 4 * tok_rows // experts
    room = 3 * capacity // (2 * dp_count)
    half = experts // 2
    chunks = CHUNKS
    width = model_width // chunks
    all_rows = dp_count * room
    far = max(chips - 1, 1)
    in_any = pl.BlockSpec(memory_space=pl.ANY)
    dma = pltpu.SemaphoreType.DMA
    return pl.pallas_call(
        functools.partial(kernel, experts, chips, chunks),
        out_shape=jax.ShapeDtypeStruct((tok_rows, model_width), BF16),
        in_specs=[in_any] * 7,
        out_specs=pl.BlockSpec(memory_space=pltpu.VMEM),
        scratch_shapes=[
            pltpu.VMEM((tok_rows, model_width), BF16),
            pltpu.VMEM((1, model_width), BF16),
            pltpu.VMEM((experts, model_width), BF16),
            pltpu.VMEM((experts + 8, capacity), jnp.int32),
            pltpu.VMEM((2, tok_rows, half * slots), BF16),
            pltpu.VMEM((2, half * slots, tok_rows), BF16),
            pltpu.VMEM((room, experts * slots), BF16),
            pltpu.VMEM((experts * slots, room), BF16),
            pltpu.VMEM((2, tok_rows, half * slots), BF16),
            pltpu.VMEM((2, tok_rows, half * slots), BF16),
            pltpu.VMEM((chunks, tok_rows, width), BF16),
            pltpu.VMEM((chunks, tok_rows, width), BF16),
            pltpu.VMEM((chunks, 2, half, slots, width), BF16),
            pltpu.VMEM((chunks, experts, slots, width), BF16),
            pltpu.VMEM((chunks, dp_count, room, width), BF16),
            pltpu.VMEM((model_width, ff), BF16),
            pltpu.VMEM((model_width, ff), BF16),
            pltpu.VMEM((chunks, ff, width), BF16),
            pltpu.VMEM((all_rows, ff), F32),
            pltpu.VMEM((all_rows, ff), F32),
            pltpu.VMEM((all_rows, ff), BF16),
            pltpu.VMEM((chunks, chips, room, width), BF16),
            pltpu.VMEM((chunks, far, room, width), BF16),
            pltpu.VMEM((chunks, experts, slots, width), BF16),
            pltpu.VMEM((chunks, 2, half, slots, width), BF16),
            pltpu.VMEM((chunks, tok_rows, width), BF16),
            pltpu.VMEM((chunks, tok_rows, width), BF16),
            dma((4,)),
            dma((chunks, 2)),
            dma((chunks,)),
            dma((chunks,)),
            dma((chunks,)),
            dma((chunks, 2, half)),
            dma((chunks, experts)),
            dma((chunks, chips)),
            dma((chunks, chips)),
            dma((chunks, dp_count)),
            dma((chunks, chips)),
            dma((chunks, chips)),
            dma((chunks, far)),
            dma((chunks, far)),
            dma((chunks, experts)),
            dma((chunks, 2, half)),
            dma((chunks,)),
            dma((chunks,)),
        ],
        compiler_params=pltpu.CompilerParams(
            collective_id=0, has_side_effects=True, vmem_limit_bytes=63 * 2**20
        ),
        name="moe",
    )(
        tokens, norm_gain.reshape(1, model_width), router_weight.T, selected,
        w_gate[0], w_up[0], w_down[0],
    )


def solution(mesh):
    in_specs = (
        P(("dp", "expert"), None),
        P(),
        P(),
        P("expert", None, "dp"),
        P("expert", None, "dp"),
        P("expert", "dp", None),
        P(),
    )
    out_specs = P(("dp", "expert"), None)
    return jax.shard_map(
        per_device, mesh=mesh, in_specs=in_specs, out_specs=out_specs, check_vma=False
    )
```

time: 136 us -> 113 us (0.83)
  Pallas kernels: 120 us -> 109 us
  other arithmetic: 7.5 us -> 0 us
  starting transfers between devices: 4.09 us -> 0 us
    pallas_call x2 -> x1, Pallas kernels: 120 us -> 109 us  [per_device(): pl.pallas_call(functools.partial(kernel, experts, chips, chunks), out_sha...]
    convert_element_type x5 -> x0, other arithmetic: 4.39 us -> none  [the longest x1 1.24 us: per_device(): (activations * lax.rsqrt(mean_square + 1e-06) * norm_gain.astype(F32)).as...]
    ppermute x1 -> x0, starting transfers between devices: 4.09 us -> none  [per_device(): far_probs = lax.ppermute(gate_probs, 'expert', swap)]
    dynamic_slice x2 -> x0, local copies, waits for them, and re-layouts: 1.52 us -> none  [the longest x1 0.76 us: per_device(): lax.dynamic_index_in_dim(selected, expert_index, 0, keepdims=False)]
    reduce_sum x2 -> x0, other arithmetic: 1.44 us -> none  [the longest x1 1.23 us: per_device(): mean_square = jnp.mean(activations * activations, axis=1, keepdims=True)]
  transfers between devices with their start and end apart: 1 -> 0, of which waited for: 0 -> 0; matrix products, arithmetic and copies ran while one was open for 4% -> 0% of each run, Pallas kernels for 46% -> 0%
where the time goes in v1:
time: 113 us; the launch traced here: 112 us
  Pallas kernels  109 us (96%)
  local copies, waits for them, and re-layouts  3.17 us (3%)
    pallas_call x1, Pallas kernels, per_device(): pl.pallas_call(functools.partial(kernel, experts, chips, chunks), out_sha...  109 us

profile of v1, /device:TPU:0, one launch (start us, length us, event | category | flops | bytes accessed | tf_op | source)
XLA Modules:
  0.0 112.3 jit_solution(15239555926067690215)
XLA Ops:
  0.0 1.3 %reshape.3.gain_hbm = bf16[1,2048]{1,0:T(2,128)(2,1)} reshape(bf16[2048]{0:T(1024)(128)(2,1)} %param.8) | data formatting | bytes 8192 | tf_op jit(solution)/shard_map/reshape | solution.py:518
  1.3 109.1 %moe.1 = bf16[128,2048]{1,0:T(8,128)(2,1)} custom-call(bf16[128,2048]{1,0:T(8,128)(2,1)} %tokens_hbm.1, bf16[1,2048]{1,0:T(2,128)(2,1)} %reshape.3.gain_hbm, bf16[8,2048]{1,0:T(8,128)(2,1)} %bitcast.7, s32[8,896]{1,0:T(8,128)} %selected_hbm.1, bf16[2048,1280]{1,0:T(8,128)(2,1)} %bitcast.4, bf16[2048,1280]{1,0:T(8,128)(2,1)} %bitcast.5, ...), custom_call_target="tpu_custom_call" | custom-call | tf_op jit(solution)/shard_map/moe/pallas_call | solution.py:461
  110.4 1.9 %copy.9 = bf16[128,2048]{1,0:T(8,128)(2,1)} copy(bf16[128,2048]{1,0:T(8,128)(2,1)} %moe.1) | data formatting | bytes 1048576

commit v2 on v1

--- a/solution.py
+++ b/solution.py
@@ -12,6 +12,7 @@
 BF16 = jnp.bfloat16
 CHUNKS = 8
 AHEAD = 2
+OWN_SLOTS = 4
 NEAR_LAG, CHIP_LAG, CORE_LAG = 2, 2, 1
 SIB_LAG, X_LAG, BACK_LAG, PAIR_LAG = 1, 2, 2, 2
 
@@ -43,16 +44,15 @@
     tokens_hbm, gain_hbm, router_hbm, selected_hbm, wg_hbm, wu_hbm, wd_hbm, out,
     tokens, gain, router, selected, chosen, pick, pack, unpack, mix_high, mix_low,
     tok_out, tok_in, outgoing, received, rows, wg, wu, wd, acc_g, acc_u, hidden,
-    sib_in, x_in, returning, arrived, back_out, back_in,
+    own, sib_in, x_in, returning, arrived, back_out, back_in,
     i_sem, w_sem, d_sem, t_send, t_recv, a_send, a_recv, x_send, s_send, b_recv,
     c_send, c_recv, o_send, o_recv, r_send, r_recv, p_send, p_recv,
 ):
     half = experts // 2
-    dp_count = 2 * chips
     tok_rows = tokens.shape[0]
     width = tok_out.shape[2]
     slots = received.shape[2]
-    room = rows.shape[2]
+    room = rows.shape[3]
     capacity = selected.shape[1]
     ff = wg.shape[1]
     tile = tile_of(ff)
@@ -122,7 +122,7 @@
     for k in range(chunks):
         part = slice(k * width, (k + 1) * width)
         tok_out[k] = (
-            tokens[:, part].astype(F32) * scale * gain[:, part].astype(F32)
+            tokens[:, part].astype(F32) * scale * gain[part].reshape(1, width).astype(F32)
         ).astype(BF16)
     pl.semaphore_wait(barrier, half + chips)
 
@@ -150,31 +150,36 @@
     def to_chip(k, i):
         other = 2 * ((chip + i) % chips) + core
         return remote(
-            rows.at[k, dp], rows.at[k, dp], x_send.at[k, i], b_recv.at[k, dp], dp=other
+            rows.at[k, core, chip], rows.at[k, core, chip],
+            x_send.at[k, i], b_recv.at[k, core, chip], dp=other,
         )
 
     def from_chip(k, i):
-        other = 2 * ((chip + i) % chips) + core
-        return remote(
-            rows.at[k, other], rows.at[k, other], x_send.at[k, i], b_recv.at[k, other], dp=other
+        other = (chip + i) % chips
+        return remote(
+            rows.at[k, core, other], rows.at[k, core, other],
+            x_send.at[k, i], b_recv.at[k, core, other], dp=2 * other + core,
         )
 
     def to_sibling(k, i):
-        block = 2 * ((chip + i) % chips) + core
-        return remote(
-            rows.at[k, block], rows.at[k, block], s_send.at[k, i], b_recv.at[k, block],
-            dp=sibling,
+        block = (chip + i) % chips
+        return remote(
+            rows.at[k, core, block], rows.at[k, core, block],
+            s_send.at[k, i], b_recv.at[k, core, block], dp=sibling,
         )
 
     def from_sibling(k, i):
-        block = 2 * ((chip + i) % chips) + 1 - core
-        return remote(
-            rows.at[k, block], rows.at[k, block], s_send.at[k, i], b_recv.at[k, block],
-            dp=sibling,
-        )
-
-    for k in range(min(AHEAD, chunks)):
-        to_partner(k).start()
+        block = (chip + i) % chips
+        return remote(
+            rows.at[k, 1 - core, block], rows.at[k, 1 - core, block],
+            s_send.at[k, i], b_recv.at[k, 1 - core, block], dp=sibling,
+        )
+
+    @pl.when(core == 0)
+    def _():
+        for k in range(min(AHEAD, chunks)):
+            to_partner(k).start()
+
     loads[2].wait()
     loads[3].wait()
 
@@ -195,7 +200,7 @@
         pick[side] = total.T.astype(BF16)
 
     def send_rows(k, side, source):
-        picked = jnp.dot(pick[side], source, preferred_element_type=F32)
+        picked = jnp.dot(pick[side], source[k], preferred_element_type=F32)
         outgoing[k, side] = picked.astype(BF16).reshape(half, slots, width)
 
         def send(i, carry):
@@ -206,7 +211,11 @@
         received[k, (me + side * half) % experts] = outgoing[k, side, local]
 
     choose(0)
-    send_rows(0, 0, tok_out[0])
+
+    @pl.when(core == 0)
+    def _():
+        send_rows(0, 0, tok_out)
+
     choose(1)
 
     mine = selected[pl.ds(me, 1), :]
@@ -246,18 +255,85 @@
         mix_high[side] = high
         mix_low[side] = (mixing - high.astype(F32)).astype(BF16)
 
+    def sib_copy(k, i):
+        return remote(
+            rows.at[k, 1 - core, i], sib_in.at[k, i], c_send.at[k, i], c_recv.at[k, i], dp=sibling
+        )
+
+    def chip_copy(k, i):
+        return remote(
+            rows.at[k, core, i - 1], x_in.at[k, i - 1],
+            o_send.at[k, i - 1], o_recv.at[k, i - 1],
+            dp=2 * ((chip + i) % chips) + core,
+        )
+
+    def give_back(k, side, i):
+        near = (local + i) % half
+        owner = (base + near + side * half) % experts
+        return remote(
+            returning.at[k, owner], arrived.at[k, side, local],
+            r_send.at[k, owner], r_recv.at[k, side, local], expert=base + near,
+        )
+
+    def take_back(k, side, i):
+        near = (local + i) % half
+        owner = (base + near + side * half) % experts
+        return remote(
+            returning.at[k, owner], arrived.at[k, side, near],
+            r_send.at[k, owner], r_recv.at[k, side, near], expert=base + near,
+        )
+
+    def pair_copy(k):
+        return remote(
+            back_out.at[k], back_in.at[k], p_send.at[k], p_recv.at[k], expert=partner
+        )
+
+    def mixed(k, side):
+        values = arrived[k, side].reshape(half * slots, width)
+        sums = jnp.dot(mix_high[side], values, preferred_element_type=F32)
+        return sums + jnp.dot(mix_low[side], values, preferred_element_type=F32)
+
+    def take_side(k, side):
+        def take(i, carry):
+            take_back(k, side, i).wait_recv()
+            return carry
+
+        lax.fori_loop(1, half, take, 0)
+
+    def when(k, *more):
+        fits = jnp.logical_and(k >= 0, k < chunks)
+        for condition in more:
+            fits = jnp.logical_and(fits, condition)
+        return pl.when(fits)
+
     lag_x = NEAR_LAG + CHIP_LAG
     lag_m = lag_x + CORE_LAG
-    for step in range(chunks + lag_m):
-        if step < chunks:
-            to_partner(step).wait_recv()
-            send_rows(step, 1, tok_in[step])
-        if step + AHEAD < chunks:
-            to_partner(step + AHEAD).start()
-        if step + 1 < chunks:
-            send_rows(step + 1, 0, tok_out[step + 1])
-        if NEAR_LAG <= step < chunks + NEAR_LAG:
-            k = step - NEAR_LAG
+    lag_w = lag_m + chunks
+    lag_t = SIB_LAG + X_LAG
+    lag_b = lag_t + BACK_LAG
+    lag_p = lag_b + PAIR_LAG
+    group_rows = chips * room
+
+    def step(t, carry):
+        s = t - core * chunks
+        r = s - lag_w
+
+        @when(s)
+        def _():
+            to_partner(s).wait_recv()
+            send_rows(s, 1, tok_in)
+
+        @when(s + AHEAD)
+        def _():
+            to_partner(s + AHEAD).start()
+
+        @when(s + 1)
+        def _():
+            send_rows(s + 1, 0, tok_out)
+
+        @when(s - NEAR_LAG)
+        def _():
+            k = s - NEAR_LAG
 
             def take(i, carry):
                 from_expert(k, 0, i).wait_recv()
@@ -270,135 +346,36 @@
                 received[k].reshape(experts * slots, width),
                 preferred_element_type=F32,
             )
-            rows[k, dp] = packed.astype(BF16)
+            rows[k, core, chip] = packed.astype(BF16)
             for i in range(1, chips):
                 to_chip(k, i).start()
             to_sibling(k, 0).start()
-        if lag_x <= step < chunks + lag_x:
-            k = step - lag_x
+
+        @when(s - lag_x)
+        def _():
+            k = s - lag_x
             for i in range(1, chips):
                 from_chip(k, i).wait_recv()
                 to_sibling(k, i).start()
-        if step == chunks:
-            weigh(0, tok_out)
-            weigh(1, tok_in)
-        if step >= lag_m:
-            k = step - lag_m
-            for i in range(chips):
-                from_sibling(k, i).wait_recv()
-            for copy in weights(k):
-                copy.wait()
-
-            def multiply(n, carry):
-                cols = pl.ds(pl.multiple_of(n * tile, tile), tile)
-                depth = pl.ds(k * width, width)
-                block = rows[k].reshape(dp_count * room, width)
-                g = jnp.dot(block, wg[depth, cols], preferred_element_type=F32)
-                u = jnp.dot(block, wu[depth, cols], preferred_element_type=F32)
-                if k > 0:
-                    g = g + acc_g[:, cols]
-                    u = u + acc_u[:, cols]
-                if k < chunks - 1:
-                    acc_g[:, cols] = g
-                    acc_u[:, cols] = u
-                else:
-                    hidden[:, cols] = (jax.nn.gelu(g, approximate=True) * u).astype(BF16)
-                return carry
-
-            lax.fori_loop(0, ff // tile, multiply, 0)
-
-    places = ff // width
-
-    def own(k, i):
-        at = k % (2 * places)
-        row = ((at // places) * chips + i) * room
-        return acc_g.at[pl.ds(row, room), pl.ds((at % places) * width, width)]
-
-    def sib_copy(k, i):
-        return remote(
-            rows.at[k, i], sib_in.at[k, i], c_send.at[k, i], c_recv.at[k, i], dp=sibling
-        )
-
-    def chip_copy(k, i):
-        return remote(
-            rows.at[k, chips + i - 1], x_in.at[k, i - 1],
-            o_send.at[k, i - 1], o_recv.at[k, i - 1],
-            dp=2 * ((chip + i) % chips) + core,
-        )
-
-    def give_back(k, side, i):
-        near = (local + i) % half
-        owner = (base + near + side * half) % experts
-        return remote(
-            returning.at[k, owner], arrived.at[k, side, local],
-            r_send.at[k, owner], r_recv.at[k, side, local], expert=base + near,
-        )
-
-    def take_back(k, side, i):
-        near = (local + i) % half
-        owner = (base + near + side * half) % experts
-        return remote(
-            returning.at[k, owner], arrived.at[k, side, near],
-            r_send.at[k, owner], r_recv.at[k, side, near], expert=base + near,
-        )
-
-    def pair_copy(k):
-        return remote(
-            back_out.at[k], back_in.at[k], p_send.at[k], p_recv.at[k], expert=partner
-        )
-
-    def mixed(k, side):
-        values = arrived[k, side].reshape(half * slots, width)
-        sums = jnp.dot(mix_high[side], values, preferred_element_type=F32)
-        return sums + jnp.dot(mix_low[side], values, preferred_element_type=F32)
-
-    def take_side(k, side):
-        def take(i, carry):
-            take_back(k, side, i).wait_recv()
-            return carry
-
-        lax.fori_loop(1, half, take, 0)
-
-    def block_rows(block):
-        return hidden[pl.ds(pl.multiple_of(block * room, 16), room), :]
-
-    lag_t = SIB_LAG + X_LAG
-    lag_b = lag_t + BACK_LAG
-    lag_p = lag_b + PAIR_LAG
-    for step in range(chunks + lag_p):
-        if step < chunks:
-            k = step
-            down_weights(k).wait()
+
+        @when(r - SIB_LAG)
+        def _():
+            k = r - SIB_LAG
             for i in range(1, chips):
                 to_chip(k, i).wait_send()
             for i in range(chips):
                 to_sibling(k, i).wait_send()
-
-            def give(i, carry):
-                block = 2 * ((chip + i) % chips) + 1 - core
-                term = jnp.dot(block_rows(block), wd[k], preferred_element_type=F32)
-                rows[k, i] = term.astype(BF16)
-                sib_copy(k, i).start()
-                return carry
-
-            lax.fori_loop(0, chips, give, 0)
-
-            def keep(i, carry):
-                block = 2 * ((chip + i) % chips) + core
-                own(k, i)[...] = jnp.dot(block_rows(block), wd[k], preferred_element_type=F32)
-                return carry
-
-            lax.fori_loop(0, chips, keep, 0)
-        if SIB_LAG <= step < chunks + SIB_LAG:
-            k = step - SIB_LAG
             for i in range(chips):
                 sib_copy(k, i).wait_recv()
             for i in range(1, chips):
-                rows[k, chips + i - 1] = (own(k, i)[...] + sib_in[k, i].astype(F32)).astype(BF16)
+                term = own[k % OWN_SLOTS, i] + sib_in[k, i].astype(F32)
+                rows[k, core, i - 1] = term.astype(BF16)
                 chip_copy(k, i).start()
-        if lag_t <= step < chunks + lag_t:
-            k = step - lag_t
-            total = own(k, 0)[...] + sib_in[k, 0].astype(F32)
+
+        @when(r - lag_t)
+        def _():
+            k = r - lag_t
+            total = own[k % OWN_SLOTS, 0] + sib_in[k, 0].astype(F32)
             for i in range(1, chips):
                 chip_copy(k, i).wait_recv()
                 total = total + x_in[k, i - 1].astype(F32)
@@ -412,20 +389,107 @@
 
                 lax.fori_loop(1, half, send, 0)
                 arrived[k, side, local] = returning[k, (me + side * half) % experts]
-        if lag_b <= step < chunks + lag_b:
-            k = step - lag_b
+
+        @when(r - lag_b)
+        def _():
+            k = r - lag_b
             take_side(k, 1)
             back_out[k] = mixed(k, 1).astype(BF16)
             pair_copy(k).start()
-        if step >= lag_p:
-            k = step - lag_p
+
+        @when(r - lag_p)
+        def _():
+            k = r - lag_p
             take_side(k, 0)
             near_sum = mixed(k, 0)
             pair_copy(k).wait_recv()
             combined = near_sum + back_in[k].astype(F32)
-            out[:, k * width : (k + 1) * width] = combined.astype(BF16)
-
-    for k in range(chunks):
+            out[:, pl.ds(pl.multiple_of(k * width, width), width)] = combined.astype(BF16)
+
+        @pl.when(s == chunks)
+        def _():
+            weigh(0, tok_out)
+            weigh(1, tok_in)
+
+        w = t - lag_w
+        w_group, w_chunk = w // chunks, w % chunks
+
+        @pl.when(jnp.logical_and(w >= 0, w < chunks))
+        def _():
+            down_weights(w_chunk).wait()
+
+        def term_of(i):
+            block = (chip + i) % chips
+            part = pl.ds(pl.multiple_of(block * room, 16), room)
+            return jnp.dot(hidden[w_group, part, :], wd[w_chunk], preferred_element_type=F32)
+
+        @pl.when(jnp.logical_and(w >= 0, w_group == 1 - core))
+        def _():
+            def give(i, carry):
+                rows[w_chunk, 1 - core, i] = term_of(i).astype(BF16)
+                sib_copy(w_chunk, i).start()
+                return carry
+
+            lax.fori_loop(0, chips, give, 0)
+
+        @pl.when(jnp.logical_and(w >= 0, w_group == core))
+        def _():
+            def keep(i, carry):
+                own[w_chunk % OWN_SLOTS, i] = term_of(i)
+                return carry
+
+            lax.fori_loop(0, chips, keep, 0)
+
+        m = t - lag_m
+        group, k = m // chunks, m % chunks
+        busy = jnp.logical_and(m >= 0, m < 2 * chunks)
+
+        @pl.when(jnp.logical_and(busy, group == 1 - core))
+        def _():
+            for i in range(chips):
+                from_sibling(k, i).wait_recv()
+
+        @pl.when(jnp.logical_and(busy, group == 0))
+        def _():
+            for copy in weights(k):
+                copy.wait()
+
+        def multiply(first, last):
+            def columns(n, carry):
+                cols = pl.ds(pl.multiple_of(n * tile, tile), tile)
+                depth = pl.ds(pl.multiple_of(k * width, width), width)
+                block = rows[k, group].reshape(group_rows, width)
+                g = jnp.dot(block, wg[depth, cols], preferred_element_type=F32)
+                u = jnp.dot(block, wu[depth, cols], preferred_element_type=F32)
+                if not first:
+                    g = g + acc_g[:, cols]
+                    u = u + acc_u[:, cols]
+                if not last:
+                    acc_g[:, cols] = g
+                    acc_u[:, cols] = u
+                else:
+                    hidden[group, :, cols] = (jax.nn.gelu(g, approximate=True) * u).astype(BF16)
+                return carry
+
+            lax.fori_loop(0, ff // tile, columns, 0)
+
+        @pl.when(jnp.logical_and(busy, k == 0))
+        def _():
+            multiply(True, chunks == 1)
+
+        @pl.when(jnp.logical_and(busy, jnp.logical_and(k > 0, k < chunks - 1)))
+        def _():
+            multiply(False, False)
+
+        @pl.when(jnp.logical_and(busy, jnp.logical_and(k > 0, k == chunks - 1)))
+        def _():
+            multiply(False, True)
+
+        return carry
+
+    lax.fori_loop(0, lag_w + 2 * chunks + lag_p, step, 0)
+
+    def finish(k, carry):
         to_partner(k).wait_send()
 
         def sent(i, carry):
@@ -440,6 +504,9 @@
         for i in range(1, chips):
             chip_copy(k, i).wait_send()
         pair_copy(k).wait_send()
+        return carry
+
+    lax.fori_loop(0, chunks, finish, 0)
 
 
 def per_device(tokens, norm_gain, router_weight, w_gate, w_up, w_down, selected):
@@ -454,7 +521,6 @@
     half = experts // 2
     chunks = CHUNKS
     width = model_width // chunks
-    all_rows = dp_count * room
     far = max(chips - 1, 1)
     in_any = pl.BlockSpec(memory_space=pl.ANY)
     dma = pltpu.SemaphoreType.DMA
@@ -465,7 +531,7 @@
         out_specs=pl.BlockSpec(memory_space=pltpu.VMEM),
         scratch_shapes=[
             pltpu.VMEM((tok_rows, model_width), BF16),
-            pltpu.VMEM((1, model_width), BF16),
+            pltpu.VMEM((model_width,), BF16),
             pltpu.VMEM((experts, model_width), BF16),
             pltpu.VMEM((experts + 8, capacity), jnp.int32),
             pltpu.VMEM((2, tok_rows, half * slots), BF16),
@@ -478,13 +544,14 @@
             pltpu.VMEM((chunks, tok_rows, width), BF16),
             pltpu.VMEM((chunks, 2, half, slots, width), BF16),
             pltpu.VMEM((chunks, experts, slots, width), BF16),
-            pltpu.VMEM((chunks, dp_count, room, width), BF16),
+            pltpu.VMEM((chunks, 2, chips, room, width), BF16),
             pltpu.VMEM((model_width, ff), BF16),
             pltpu.VMEM((model_width, ff), BF16),
             pltpu.VMEM((chunks, ff, width), BF16),
-            pltpu.VMEM((all_rows, ff), F32),
-            pltpu.VMEM((all_rows, ff), F32),
-            pltpu.VMEM((all_rows, ff), BF16),
+            pltpu.VMEM((chips * room, ff), F32),
+            pltpu.VMEM((chips * room, ff), F32),
+            pltpu.VMEM((2, chips * room, ff), BF16),
+            pltpu.VMEM((OWN_SLOTS, chips, room, width), F32),
             pltpu.VMEM((chunks, chips, room, width), BF16),
             pltpu.VMEM((chunks, far, room, width), BF16),
             pltpu.VMEM((chunks, experts, slots, width), BF16),
@@ -500,7 +567,7 @@
             dma((chunks, experts)),
             dma((chunks, chips)),
             dma((chunks, chips)),
-            dma((chunks, dp_count)),
+            dma((chunks, 2, chips)),
             dma((chunks, chips)),
             dma((chunks, chips)),
             dma((chunks, far)),
@@ -515,7 +582,7 @@
         ),
         name="moe",
     )(
-        tokens, norm_gain.reshape(1, model_width), router_weight.T, selected,
+        tokens, norm_gain, router_weight.T, selected,
         w_gate[0], w_up[0], w_down[0],
     )
 

time: 113 us -> 106 us (0.938)
  the two profiles are of different devices: /device:TPU:0 before, /device:TPU:1 now
where the time goes in v2:
time: 106 us; the launch traced here: 105 us
  Pallas kernels  104 us (98%)
  local copies, waits for them, and re-layouts  1.88 us (2%)
    pallas_call x1, Pallas kernels, per_device(): pl.pallas_call(functools.partial(kernel, experts, chips, chunks), out_sha...  104 us

profile of v2, /device:TPU:1, one launch (start us, length us, event | category | flops | bytes accessed | tf_op | source)
XLA Modules:
  0.0 105.5 jit_solution(11765196341272215792)
XLA Ops:
  0.0 103.6 %moe.1 = bf16[128,2048]{1,0:T(8,128)(2,1)} custom-call(bf16[128,2048]{1,0:T(8,128)(2,1)} %tokens_hbm.1, bf16[2048]{0:T(1024)(128)(2,1)} %gain_hbm.1, bf16[8,2048]{1,0:T(8,128)(2,1)} %bitcast.7, s32[8,896]{1,0:T(8,128)} %selected_hbm.1, bf16[2048,1280]{1,0:T(8,128)(2,1)} %bitcast.4, bf16[2048,1280]{1,0:T(8,128)(2,1)} %bitcast.5, bf16[1280,2048]{1,0:T(8,128)(2,1)} %bitcast.6), custom_call_target="tpu_custom_call" | custom-call | tf_op jit(solution)/shard_map/moe/pallas_call | solution.py:527
  103.6 1.9 %copy.9 = bf16[128,2048]{1,0:T(8,128)(2,1)} copy(bf16[128,2048]{1,0:T(8,128)(2,1)} %moe.1) | data formatting | bytes 1048576

commit v3 on v2

--- a/solution.py
+++ b/solution.py
@@ -14,7 +14,7 @@
 AHEAD = 2
 OWN_SLOTS = 4
 NEAR_LAG, CHIP_LAG, CORE_LAG = 2, 2, 1
-SIB_LAG, X_LAG, BACK_LAG, PAIR_LAG = 1, 2, 2, 2
+SIB_LAG, X_LAG, BACK_LAG, PAIR_LAG = 1, 2, 2, 3
 
 
 def tile_of(width):
@@ -175,7 +175,7 @@
             s_send.at[k, i], b_recv.at[k, 1 - core, block], dp=sibling,
         )
 
-    @pl.when(core == 0)
+    @pl.when(core == 1)
     def _():
         for k in range(min(AHEAD, chunks)):
             to_partner(k).start()
@@ -212,7 +212,7 @@
 
     choose(0)
 
-    @pl.when(core == 0)
+    @pl.when(core == 1)
     def _():
         send_rows(0, 0, tok_out)
 
@@ -315,7 +315,7 @@
     group_rows = chips * room
 
     def step(t, carry):
-        s = t - core * chunks
+        s = t - (1 - core) * chunks
         r = s - lag_w
 
         @when(s)
@@ -412,7 +412,7 @@
             weigh(1, tok_in)
 
         w = t - lag_w
-        w_group, w_chunk = w // chunks, w % chunks
+        w_group, w_chunk = 1 - w // chunks, w % chunks
 
         @pl.when(jnp.logical_and(w >= 0, w < chunks))
         def _():
@@ -441,7 +441,8 @@
             lax.fori_loop(0, chips, keep, 0)
 
         m = t - lag_m
-        group, k = m // chunks, m % chunks
+        turn, k = m // chunks, m % chunks
+        group = 1 - turn
         busy = jnp.logical_and(m >= 0, m < 2 * chunks)
 
         @pl.when(jnp.logical_and(busy, group == 1 - core))
@@ -449,7 +450,7 @@
             for i in range(chips):
                 from_sibling(k, i).wait_recv()
 
-        @pl.when(jnp.logical_and(busy, group == 0))
+        @pl.when(jnp.logical_and(busy, turn == 0))
         def _():
             for copy in weights(k):
                 copy.wait()

time: 106 us -> 103 us (0.972)
  the two profiles are of different devices: /device:TPU:1 before, /device:TPU:0 now
where the time goes in v3:
time: 103 us
  Pallas kernels  101 us (98%)
  local copies, waits for them, and re-layouts  1.88 us (2%)
    pallas_call x1, Pallas kernels, per_device(): pl.pallas_call(functools.partial(kernel, experts, chips, chunks), out_sha...  101 us

profile of v3, /device:TPU:0, one launch (start us, length us, event | category | flops | bytes accessed | tf_op | source)
XLA Modules:
  0.0 102.6 jit_solution(10872544805470724998)
XLA Ops:
  0.0 100.7 %moe.1 = bf16[128,2048]{1,0:T(8,128)(2,1)} custom-call(bf16[128,2048]{1,0:T(8,128)(2,1)} %tokens_hbm.1, bf16[2048]{0:T(1024)(128)(2,1)} %gain_hbm.1, bf16[8,2048]{1,0:T(8,128)(2,1)} %bitcast.7, s32[8,896]{1,0:T(8,128)} %selected_hbm.1, bf16[2048,1280]{1,0:T(8,128)(2,1)} %bitcast.4, bf16[2048,1280]{1,0:T(8,128)(2,1)} %bitcast.5, bf16[1280,2048]{1,0:T(8,128)(2,1)} %bitcast.6), custom_call_target="tpu_custom_call" | custom-call | tf_op jit(solution)/shard_map/moe/pallas_call | solution.py:528
  100.7 1.9 %copy.9 = bf16[128,2048]{1,0:T(8,128)(2,1)} copy(bf16[128,2048]{1,0:T(8,128)(2,1)} %moe.1) | data formatting | bytes 1048576

commit v4 on v3

--- a/solution.py
+++ b/solution.py
@@ -223,18 +223,24 @@
     firsts = jnp.sum(jnp.where(mine < starts, 1.0, 0.0), axis=1, keepdims=True)
     place = iota((1, experts * slots), 1).astype(F32)
     target = jnp.full((1, experts * slots), -1.0, F32)
-    slot = iota((slots, 1), 0).astype(F32)
-    seats = iota((1, room), 1).astype(F32)
     for j in range(experts):
         offset = firsts[j : j + 1] - firsts[0:1]
         count = firsts[j + 1 : j + 2] - firsts[j : j + 1]
         within = place - float(j * slots)
         here = jnp.logical_and(within >= 0.0, within < count)
         target = jnp.where(here, within + offset, target)
-        goal = jnp.where(slot < count, slot + offset, -1.0)
-        unpack[j * slots : (j + 1) * slots, :] = jnp.where(goal == seats, 1.0, 0.0).astype(BF16)
     seat = iota((room, 1), 0).astype(F32)
     pack[...] = jnp.where(seat == target, 1.0, 0.0).astype(BF16)
+
+    def place_back():
+        slot = iota((slots, 1), 0).astype(F32)
+        seats = iota((1, room), 1).astype(F32)
+        for j in range(experts):
+            offset = firsts[j : j + 1] - firsts[0:1]
+            count = firsts[j + 1 : j + 2] - firsts[j : j + 1]
+            goal = jnp.where(slot < count, slot + offset, -1.0)
+            part = slice(j * slots, (j + 1) * slots)
+            unpack[part, :] = jnp.where(goal == seats, 1.0, 0.0).astype(BF16)
 
     def weigh(side, source):
         logits = jnp.zeros((tok_rows, experts), F32)
@@ -318,11 +324,6 @@
         s = t - (1 - core) * chunks
         r = s - lag_w
 
-        @when(s)
-        def _():
-            to_partner(s).wait_recv()
-            send_rows(s, 1, tok_in)
-
         @when(s + AHEAD)
         def _():
             to_partner(s + AHEAD).start()
@@ -357,6 +358,11 @@
             for i in range(1, chips):
                 from_chip(k, i).wait_recv()
                 to_sibling(k, i).start()
+
+        @when(s)
+        def _():
+            to_partner(s).wait_recv()
+            send_rows(s, 1, tok_in)
 
         @when(r - SIB_LAG)
         def _():
@@ -408,6 +414,7 @@
 
         @pl.when(s == chunks)
         def _():
+            place_back()
             weigh(0, tok_out)
             weigh(1, tok_in)
 

time: 103 us -> 103 us (level)
  no operation moved by 1% of the time
where the time goes in v4:
time: 103 us; the launch traced here: 102 us
  Pallas kernels  101 us (98%)
  local copies, waits for them, and re-layouts  1.88 us (2%)
    pallas_call x1, Pallas kernels, per_device(): pl.pallas_call(functools.partial(kernel, experts, chips, chunks), out_sha...  101 us

profile of v4, /device:TPU:0, one launch (start us, length us, event | category | flops | bytes accessed | tf_op | source)
XLA Modules:
  0.0 102.4 jit_solution(14728074392374241297)
XLA Ops:
  0.0 100.5 %moe.1 = bf16[128,2048]{1,0:T(8,128)(2,1)} custom-call(bf16[128,2048]{1,0:T(8,128)(2,1)} %tokens_hbm.1, bf16[2048]{0:T(1024)(128)(2,1)} %gain_hbm.1, bf16[8,2048]{1,0:T(8,128)(2,1)} %bitcast.7, s32[8,896]{1,0:T(8,128)} %selected_hbm.1, bf16[2048,1280]{1,0:T(8,128)(2,1)} %bitcast.4, bf16[2048,1280]{1,0:T(8,128)(2,1)} %bitcast.5, bf16[1280,2048]{1,0:T(8,128)(2,1)} %bitcast.6), custom_call_target="tpu_custom_call" | custom-call | tf_op jit(solution)/shard_map/moe/pallas_call | solution.py:535
  100.5 1.9 %copy.9 = bf16[128,2048]{1,0:T(8,128)(2,1)} copy(bf16[128,2048]{1,0:T(8,128)(2,1)} %moe.1) | data formatting | bytes 1048576
